TPU v7x, 32 devices: a whole 2x2x4 slice. The times are simulated.
32 devices in a mesh: groups: 2 (over y), cells: 8 (over z, x), side: 2 (over core).
Axes of the slice: x: 2, y: 2, z: 4, core: 2. Of those that a mesh axis runs over, the one named last changes fastest.
Arguments:
- datasets: float32 [2, 2000, 8192], P('side', None, ('groups', 'cells')), parts along dimension 2, may hold values from -6 to 6
- sketch: float32 [64, 8192], P(None, ('groups', 'cells')), parts along dimension 1, may hold values from -6 to 6
Outputs:
- factors: float32 [2, 64, 8192], P('side', None, ('groups', 'cells')), parts along dimension 2
There are 2 independent parts, one for each index of `groups`. A program takes and returns all parts, laid end to end along the dimension named above; each array names one. Nothing has to cross between parts.
All inputs are finite; a program needn't handle non-finite values.
Results may differ from a plain program's by a relative error of at most 0.00009.
Values sent between devices are 32-bit elements; how exact they have to be, the bound alone decides.
A program may use at most 64 MiB of HBM per device.

v0:
```python
import jax
import jax.numpy as jnp
from jax import lax
from jax.sharding import PartitionSpec as P


def from_behind(value, axis, steps):
    count = lax.axis_size(axis)
    initial, last = (max(0, -steps), min(count, count - steps))
    return lax.ppermute(value, axis, [(source, source + steps) for source in range(initial, last)])


def per_device(datasets, sketch):
    high = lax.Precision.HIGHEST
    own_data = datasets[0]
    side_index = lax.axis_index("side")
    cell_count = own_data.shape[1] * lax.axis_size("cells")
    scale = jnp.sqrt(jnp.float32(cell_count))
    partial_value = jnp.dot(sketch, own_data.T, precision=high)
    summed = lax.psum(partial_value, "cells")
    arrived = from_behind(summed, "side", -1)
    panel = jnp.where(side_index == 0, arrived, summed)
    range_rows = jnp.dot(panel, own_data, precision=high)
    gram_part = jnp.dot(range_rows, range_rows.T, precision=high)
    raw_part = jnp.dot(range_rows, own_data.T, precision=high)
    gram, raw_cross = lax.psum((gram_part, raw_part), "cells")
    lower = jnp.linalg.cholesky(gram)
    basis = jax.scipy.linalg.solve_triangular(lower, range_rows, lower=True)
    cross = jax.scipy.linalg.solve_triangular(lower, raw_cross, lower=True)
    received = from_behind(cross, "side", 1)
    projected = jnp.dot(received, own_data, precision=high)
    result = jnp.where(side_index == 0, basis * scale, projected / scale)
    return result[None]


def solution(mesh):
    in_specs = (P("side", None, ("groups", "cells")), P(None, ("groups", "cells")))
    out_specs = P("side", None, ("groups", "cells"))
    return jax.shard_map(
        per_device, mesh=mesh, in_specs=in_specs, out_specs=out_specs, check_vma=False
    )
```

profile of v0, /device:TPU:0, one launch (start us, length us, event | category | flops | bytes accessed | tf_op | source)
XLA Modules:
  0.0 225.7 jit_solution(7290744189002880673)
XLA Ops:
  6.5 0.0 copy-start
  6.5 0.0 all-reduce.3.cloned.1.call-start
  6.5 0.9 copy-done
  7.4 6.7 %fusion.6 = f32[64,2000]{1,0:T(8,128)} fusion(f32[64,512]{1,0:T(8,128)S(1)} %copy-done, f32[1,2000,512]{2,1,0:T(8,128)} %param.2), kind=kOutput, calls=%fused_computation.6 | convolution fusion | flops 786432000 | bytes 4739072 | tf_op jit(solution)/shard_map/dot_general | solution.py:19
  14.1 0.0 all-reduce.3.cloned.1.call-update
  14.2 0.0 all-reduce.5.cloned.1.call-start
  14.2 75.5 %all-reduce.3.cloned.1.call-done = f32[64,2000]{1,0:T(8,128)} async-done(((f32[64,2000]{1,0:T(8,128)}), f32[64,2000]{1,0:T(8,128)}) %all-reduce.3.cloned.1.call-update) | async-done | bytes 512016 | tf_op jit(solution)/shard_map/psum | solution.py:20
  89.7 1.3 collective-permute-start
  91.0 0.0 copy-start.1
  91.0 2.7 %collective-permute-done = f32[64,2000]{1,0:T(8,128)S(1)} collective-permute-done((f32[64,2000]{1,0:T(8,128)}, f32[64,2000]{1,0:T(8,128)S(1)}, u32[]{:S(2)}, u32[]{:S(2)}) %collective-permute-start) | collective-permute-done | bytes 512032 | tf_op jit(solution)/shard_map/ppermute | solution.py:10
  93.7 4.8 %fusion.4 = f32[64,512]{1,0:T(8,128)S(1)} fusion(f32[1,2000,512]{2,1,0:T(8,128)} %param.2, f32[64,2000]{1,0:T(8,128)S(1)} %collective-permute-done, f32[64,2000]{1,0:T(8,128)} %all-reduce.3.cloned.1.call-done, pred[]{:T(512)S(6)} %eq.4), kind=kOutput, calls=%fused_computation.4 | convolution fusion | flops 786560000 | bytes 5251073 | tf_op jit(solution)/shard_map/dot_general | solution.py:23
  98.5 0.3 fusion.24
  98.7 0.0 copy-done.1
  98.7 4.6 %fusion.2 = f32[64,2000]{1,0:T(8,128)} fusion(f32[64,512]{1,0:T(8,128)S(1)} %fusion.4, f32[1,2000,512]{2,1,0:T(8,128)S(1)} %copy-done.1), kind=kOutput, calls=%fused_computation.2 | convolution fusion | flops 786432000 | bytes 4739072 | tf_op jit(solution)/shard_map/dot_general | solution.py:25
  103.3 35.4 %psum.22 = f32[64,64]{0,1:T(8,128)S(1)} all-reduce(f32[64,64]{0,1:T(8,128)S(1)} %fusion.24), channel_id=1, replica_groups=mesh['groups'=2,'cells'=8,'side'=2] {'cells'}, use_global_device_ids=true, to_apply=%region_1.2 | all-reduce | flops 4096 | bytes 32768 | tf_op jit(solution)/shard_map/psum | solution.py:26
  138.7 0.1 copy.4
  138.8 0.0 all-reduce.5.cloned.1.call-update
  138.8 5.8 %cholesky.16 = f32[64,64]{1,0:T(8,128)S(1)} custom-call(f32[64,64]{1,0:T(8,128)S(1)} %fusion.23), custom_call_target="Cholesky" | custom-call | tf_op jit(solution)/shard_map/jit(cholesky)/cholesky | solution.py:27
  144.7 0.6 compare_reduce_fusion
  145.3 0.7 fusion.19
  146.0 4.9 %custom-call.10 = f32[1,64,64]{1,2,0:T(8,128)S(1)} custom-call(f32[1,64,64]{2,1,0:T(8,128)S(1)} %fusion.19), custom_call_target="InvertDiagBlocksLowerTriangular" | custom-call | tf_op jit(solution)/shard_map/jit(_solve_triangular)/triangular_solve | solution.py:28
  150.9 58.1 %all-reduce.5.cloned.1.call-done = f32[64,2000]{1,0:T(8,128)} async-done(((f32[64,2000]{1,0:T(8,128)}), f32[64,2000]{1,0:T(8,128)}) %all-reduce.5.cloned.1.call-update) | async-done | bytes 512016 | tf_op jit(solution)/shard_map/psum | solution.py:26
  209.0 1.7 fusion.20
  210.6 1.3 collective-permute-start.1
  212.0 0.3 convolution_multiply_fusion
  212.3 1.2 collective-permute-done.1
  213.5 5.4 %fusion.14 = f32[1,64,512]{2,1,0:T(8,128)} fusion(f32[64,512]{1,0:T(8,128)S(1)} %convolution_multiply_fusion, f32[64,2000]{1,0:T(8,128)S(1)} %collective-permute-done.1, f32[1,2000,512]{2,1,0:T(8,128)} %param.2, pred[]{:T(512)S(6)} %eq.4), kind=kOutput, calls=%fused_computation.10 | convolution fusion | flops 786497536 | bytes 4870145 | tf_op jit(solution)/shard_map/dot_general | solution.py:31
  (2 shorter events, 0.0 us)
Async XLA Ops:
  6.5 0.9 copy-start
  6.5 83.2 %all-reduce.3.cloned.1.call-start = ((), (), s32[]{:S(2)}) async-start(), calls=%async_computation | async-start | bytes 1048576 | tf_op jit(solution)/shard_map/psum | solution.py:20
  14.2 194.8 %all-reduce.5.cloned.1.call-start = ((), (), s32[]{:S(2)}) async-start(), calls=%async_computation.1 | async-start | bytes 1048576 | tf_op jit(solution)/shard_map/psum | solution.py:26
  89.7 4.0 %collective-permute-start = (f32[64,2000]{1,0:T(8,128)}, f32[64,2000]{1,0:T(8,128)S(1)}, u32[]{:S(2)}, u32[]{:S(2)}) collective-permute-start(f32[64,2000]{1,0:T(8,128)} %all-reduce.3.cloned.1.call-done), channel_id=1, source_target_pairs={{1,0},{3,2},{5,4},{7,6},{9,8},{11,10},{13,12},{15,14},{17,16},{19,... | collective-permute-start | bytes 1536008 | tf_op jit(solution)/shard_map/ppermute | solution.py:10
  91.0 7.7 %copy-start.1 = (f32[1,2000,512]{2,1,0:T(8,128)S(1)}, f32[1,2000,512]{2,1,0:T(8,128)}, u32[]{:S(2)}) copy-start(f32[1,2000,512]{2,1,0:T(8,128)} %param.2) | copy-start | bytes 12288004
  210.6 2.8 %collective-permute-start.1 = (f32[64,2000]{1,0:T(8,128)S(1)}, f32[64,2000]{1,0:T(8,128)S(1)}, u32[]{:S(2)}, u32[]{:S(2)}) collective-permute-start(f32[64,2000]{1,0:T(8,128)S(1)} %fusion.20), channel_id=1, source_target_pairs={{0,1},{2,3},{4,5},{6,7},{8,9},{10,11},{12,13},{14,15},{16,17},{18,... | collective-permute-start | bytes 1536008 | tf_op jit(solution)/shard_map/ppermute | solution.py:10
Sparse Core Ops, SparseCore 0:
  14.3 75.3 all-reduce.2
  138.9 70.0 all-reduce.4
where the time goes:
time: 226 us
  waiting for transfers between devices  137 us (61%)
  blocking collectives  35.4 us (16%)
  matrix products  23.7 us (10%)
  between operations  13.5 us (6%)
  other arithmetic  12.1 us (5%)
  starting transfers between devices  2.65 us (1%)
    psum x1, waiting for transfers between devices, per_device(): summed = lax.psum(partial_value, 'cells')  75.5 us
    psum x1, waiting for transfers between devices, per_device(): gram, raw_cross = lax.psum((gram_part, raw_part), 'cells')  58.1 us
    psum x1, blocking collectives, per_device(): gram, raw_cross = lax.psum((gram_part, raw_part), 'cells')  35.4 us
    dot_general x1, matrix products, per_device(): partial_value = jnp.dot(sketch, own_data.T, precision=high)  6.69 us
    another operation x3, other arithmetic, per_device(): lower = jnp.linalg.cholesky(gram)  6.52 us
    another operation x2, other arithmetic, per_device(): basis = jax.scipy.linalg.solve_triangular(lower, range_rows, lower=True)  5.55 us
    dot_general x1, matrix products, per_device(): projected = jnp.dot(received, own_data, precision=high)  5.43 us
    dot_general x1, matrix products, per_device(): range_rows = jnp.dot(panel, own_data, precision=high)  4.75 us
  transfers between devices with their start and end apart: 4, of which 4 were waited for; matrix products, arithmetic and copies ran while one was open for 5% of the time, Pallas kernels for 0%

commit v1 on v0

--- a/solution.py
+++ b/solution.py
@@ -17,7 +17,7 @@
     cell_count = own_data.shape[1] * lax.axis_size("cells")
     scale = jnp.sqrt(jnp.float32(cell_count))
     partial_value = jnp.dot(sketch, own_data.T, precision=high)
-    summed = lax.psum(partial_value, "cells")
+    summed = jnp.sum(lax.all_gather(partial_value, "cells"), axis=0)
     arrived = from_behind(summed, "side", -1)
     panel = jnp.where(side_index == 0, arrived, summed)
     range_rows = jnp.dot(panel, own_data, precision=high)

time: 226 us -> 228 us (level)
  other arithmetic: 12.1 us -> 14.6 us
    all_gather x0 -> x1, waiting for transfers between devices: none -> 75.6 us  [per_device(): summed = jnp.sum(lax.all_gather(partial_value, 'cells'), axis=0)]
    psum x1 -> x0, waiting for transfers between devices: 75.5 us -> none  [per_device(): summed = lax.psum(partial_value, 'cells')]
    reduce_sum x0 -> x1, other arithmetic: none -> 2.5 us  [per_device(): summed = jnp.sum(lax.all_gather(partial_value, 'cells'), axis=0)]
where the time goes in v1:
time: 228 us
  waiting for transfers between devices  137 us (60%)
  blocking collectives  34.7 us (15%)
  matrix products  23.7 us (10%)
  other arithmetic  14.6 us (6%)
  between operations  13.5 us (6%)
  starting transfers between devices  2.84 us (1%)
    all_gather x1, waiting for transfers between devices, per_device(): summed = jnp.sum(lax.all_gather(partial_value, 'cells'), axis=0)  75.6 us
    psum x1, waiting for transfers between devices, per_device(): gram, raw_cross = lax.psum((gram_part, raw_part), 'cells')  58 us
    psum x1, blocking collectives, per_device(): gram, raw_cross = lax.psum((gram_part, raw_part), 'cells')  34.7 us
    dot_general x1, matrix products, per_device(): partial_value = jnp.dot(sketch, own_data.T, precision=high)  6.67 us
    another operation x3, other arithmetic, per_device(): lower = jnp.linalg.cholesky(gram)  6.52 us
    another operation x2, other arithmetic, per_device(): basis = jax.scipy.linalg.solve_triangular(lower, range_rows, lower=True)  5.55 us
    dot_general x1, matrix products, per_device(): projected = jnp.dot(received, own_data, precision=high)  5.42 us
    dot_general x1, matrix products, per_device(): range_rows = jnp.dot(panel, own_data, precision=high)  4.75 us
  transfers between devices with their start and end apart: 4, of which 4 were waited for; matrix products, arithmetic and copies ran while one was open for 5% of the time, Pallas kernels for 0%

profile of v1, /device:TPU:0, one launch (start us, length us, event | category | flops | bytes accessed | tf_op | source)
XLA Modules:
  0.0 227.6 jit_solution(13135063198504549264)
XLA Ops:
  6.5 0.0 copy-start
  6.5 0.0 all-gather.3.cloned.1.call-start
  6.5 0.9 copy-done
  7.4 6.7 %fusion.6 = f32[64,2000]{1,0:T(8,128)} fusion(f32[64,512]{1,0:T(8,128)S(1)} %copy-done, f32[1,2000,512]{2,1,0:T(8,128)} %param.2), kind=kOutput, calls=%fused_computation.6 | convolution fusion | flops 786432000 | bytes 4739072 | tf_op jit(solution)/shard_map/dot_general | solution.py:19
  14.1 0.0 all-gather.3.cloned.1.call-update
  14.1 0.0 all-reduce.2.cloned.1.call-start
  14.2 75.6 %all-gather.3.cloned.1.call-done = f32[512,2000]{1,0:T(8,128)} async-done(((f32[64,2000]{1,0:T(8,128)}), f32[512,2000]{1,0:T(8,128)}) %all-gather.3.cloned.1.call-update) | async-done | bytes 4096016 | tf_op jit(solution)/shard_map/all_gather | solution.py:20
  89.8 2.5 %reduce_sum.9 = f32[64,2000]{1,0:T(8,128)S(1)} reduce(f32[8,64,2000]{2,1,0:T(8,128)} %bitcast.36, f32[]{:T(128)} %constant.54.clone.1), dimensions={0}, to_apply=%region_0.0 | reduce | flops 896000 | bytes 4608004 | tf_op jit(solution)/shard_map/reduce_sum | solution.py:20
  92.3 1.3 collective-permute-start
  93.6 0.0 copy-start.1
  93.6 2.5 %collective-permute-done = f32[64,2000]{1,0:T(8,128)S(1)} collective-permute-done((f32[64,2000]{1,0:T(8,128)S(1)}, f32[64,2000]{1,0:T(8,128)S(1)}, u32[]{:S(2)}, u32[]{:S(2)}) %collective-permute-start) | collective-permute-done | bytes 512032 | tf_op jit(solution)/shard_map/ppermute | solution.py:10
  96.1 4.7 %fusion.4 = f32[64,512]{1,0:T(8,128)S(1)} fusion(f32[1,2000,512]{2,1,0:T(8,128)} %param.2, f32[64,2000]{1,0:T(8,128)S(1)} %collective-permute-done, f32[64,2000]{1,0:T(8,128)S(1)} %reduce_sum.9, pred[]{:T(512)S(6)} %eq.4), kind=kOutput, calls=%fused_computation.4 | convolution fusion | flops 786560000 | bytes 5251073 | tf_op jit(solution)/shard_map/dot_general | solution.py:23
  100.9 0.3 fusion.24
  101.1 0.0 copy-done.1
  101.2 4.6 %fusion.2 = f32[64,2000]{1,0:T(8,128)} fusion(f32[64,512]{1,0:T(8,128)S(1)} %fusion.4, f32[1,2000,512]{2,1,0:T(8,128)S(1)} %copy-done.1), kind=kOutput, calls=%fused_computation.2 | convolution fusion | flops 786432000 | bytes 4739072 | tf_op jit(solution)/shard_map/dot_general | solution.py:25
  105.7 34.7 %psum.14 = f32[64,64]{0,1:T(8,128)S(1)} all-reduce(f32[64,64]{0,1:T(8,128)S(1)} %fusion.24), channel_id=1, replica_groups=mesh['groups'=2,'cells'=8,'side'=2] {'cells'}, use_global_device_ids=true, to_apply=%region_1.2 | all-reduce | flops 4096 | bytes 32768 | tf_op jit(solution)/shard_map/psum | solution.py:26
  140.4 0.1 copy.4
  140.5 0.0 all-reduce.2.cloned.1.call-update
  140.6 5.8 %cholesky.16 = f32[64,64]{1,0:T(8,128)S(1)} custom-call(f32[64,64]{1,0:T(8,128)S(1)} %fusion.23), custom_call_target="Cholesky" | custom-call | tf_op jit(solution)/shard_map/jit(cholesky)/cholesky | solution.py:27
  146.4 0.6 compare_reduce_fusion
  147.1 0.7 fusion.19
  147.7 4.9 %custom-call.10 = f32[1,64,64]{1,2,0:T(8,128)S(1)} custom-call(f32[1,64,64]{2,1,0:T(8,128)S(1)} %fusion.19), custom_call_target="InvertDiagBlocksLowerTriangular" | custom-call | tf_op jit(solution)/shard_map/jit(_solve_triangular)/triangular_solve | solution.py:28
  152.6 58.0 %all-reduce.2.cloned.1.call-done = f32[64,2000]{1,0:T(8,128)} async-done(((f32[64,2000]{1,0:T(8,128)}), f32[64,2000]{1,0:T(8,128)}) %all-reduce.2.cloned.1.call-update) | async-done | bytes 512016 | tf_op jit(solution)/shard_map/psum | solution.py:26
  210.7 1.7 fusion.20
  212.3 1.5 collective-permute-start.1
  213.8 0.3 convolution_multiply_fusion
  214.2 1.2 collective-permute-done.1
  215.3 5.4 %fusion.14 = f32[1,64,512]{2,1,0:T(8,128)} fusion(f32[64,512]{1,0:T(8,128)S(1)} %convolution_multiply_fusion, f32[64,2000]{1,0:T(8,128)S(1)} %collective-permute-done.1, f32[1,2000,512]{2,1,0:T(8,128)} %param.2, pred[]{:T(512)S(6)} %eq.4), kind=kOutput, calls=%fused_computation.10 | convolution fusion | flops 786497536 | bytes 4870145 | tf_op jit(solution)/shard_map/dot_general | solution.py:31
  (2 shorter events, 0.0 us)
Async XLA Ops:
  6.5 0.9 copy-start
  6.5 83.3 %all-gather.3.cloned.1.call-start = ((), (), s32[]{:S(2)}) async-start(), calls=%async_computation.1 | async-start | bytes 4718592 | tf_op jit(solution)/shard_map/all_gather | solution.py:20
  14.1 196.5 %all-reduce.2.cloned.1.call-start = ((), (), s32[]{:S(2)}) async-start(), calls=%async_computation | async-start | bytes 1048576 | tf_op jit(solution)/shard_map/psum | solution.py:26
  92.3 3.8 %collective-permute-start = (f32[64,2000]{1,0:T(8,128)S(1)}, f32[64,2000]{1,0:T(8,128)S(1)}, u32[]{:S(2)}, u32[]{:S(2)}) collective-permute-start(f32[64,2000]{1,0:T(8,128)S(1)} %reduce_sum.9), channel_id=1, source_target_pairs={{1,0},{3,2},{5,4},{7,6},{9,8},{11,10},{13,12},{15,14},{17,16},{19,... | collective-permute-start | bytes 1536008 | tf_op jit(solution)/shard_map/ppermute | solution.py:10
  93.6 7.5 %copy-start.1 = (f32[1,2000,512]{2,1,0:T(8,128)S(1)}, f32[1,2000,512]{2,1,0:T(8,128)}, u32[]{:S(2)}) copy-start(f32[1,2000,512]{2,1,0:T(8,128)} %param.2) | copy-start | bytes 12288004
  212.3 3.0 %collective-permute-start.1 = (f32[64,2000]{1,0:T(8,128)S(1)}, f32[64,2000]{1,0:T(8,128)S(1)}, u32[]{:S(2)}, u32[]{:S(2)}) collective-permute-start(f32[64,2000]{1,0:T(8,128)S(1)} %fusion.20), channel_id=1, source_target_pairs={{0,1},{2,3},{4,5},{6,7},{8,9},{10,11},{12,13},{14,15},{16,17},{18,... | collective-permute-start | bytes 1536008 | tf_op jit(solution)/shard_map/ppermute | solution.py:10
Sparse Core Ops, SparseCore 0:
  14.3 75.5 all-gather.2
  140.7 69.9 all-reduce.1
